TPU v7x, 256 devices: a whole 4x4x8 slice. The times are simulated.
256 devices in a mesh: batch: 32 (over z_hi, y, core), gene: 8 (over x, z_lo).
Axes of the slice: x: 4, y: 4, z: 8 (z_hi: 4, z_lo: 2; z = z_hi * 2 + z_lo), core: 2. Of those that a mesh axis runs over, the one named last changes fastest.
Arguments:
- umi_counts: int32 [32768, 8192], P('batch', 'gene'), may hold values from 0 to 65535
- cell_donors: int32 [32768], P('batch'), may hold values from 0 to 127
- cell_types: int32 [32768], P('batch'), may hold values from 0 to 23
- live_cells: int32 [32], P('batch'), may hold values from 1 to 1024, 20480 in all
- dosages: int32 [128, 4096], P(None, 'batch'), may hold values from 0 to 2
Outputs:
- scores: bfloat16 [24, 8192, 4096], P(None, ('gene', 'batch'))
All inputs are finite; a program needn't handle non-finite values. No bound on the sum of `live_cells` on one device may be relied on, other than what follows from the above.
Results may differ from a plain program's by a relative error of at most 0.0069.
Values may be sent and summed in bfloat16 or wider, within the bound.
A program may use at most 128 MiB of HBM per device.

v0:
```python
import jax
import jax.numpy as jnp
from jax import lax
from jax.sharding import Mesh
from jax.sharding import PartitionSpec as P

TYPES = 24
DONORS = 128
BATCH = ("batch_0", "batch_1", "batch_2")
BATCH_GENE = ("batch_0", "batch_1", "batch_2", "gene_0", "gene_1")
GENE = ("gene_0", "gene_1")
GENE_BATCH = ("gene_0", "gene_1", "batch_0", "batch_1", "batch_2")


def in_blocks(value, dim, count):
    dims = value.shape
    tiles = value.reshape(*dims[:dim], count, dims[dim] // count, *dims[dim + 1 :])
    return jnp.moveaxis(tiles, dim, 0)


def summed_rows_2(value, chips, core, dim):
    sizes = (lax.axis_size(chips), lax.axis_size(core))
    tiles = in_blocks(value, dim, sizes[0] * sizes[1])
    inside = tiles.shape[1:]
    tiles = tiles.reshape(*sizes, *inside).swapaxes(0, 1).reshape(-1, *inside)
    tiles = lax.psum_scatter(tiles, core, scatter_dimension=0, tiled=True)
    return lax.psum_scatter(tiles, chips, scatter_dimension=0, tiled=True)[0]


def one_axis_at_a_time(value, axes):
    for axis in axes:
        value = lax.psum(value, axis)
    return value


def one_hot_rows(group_ids, total_groups):
    columns = jnp.arange(total_groups, dtype=jnp.int32)
    return (group_ids[:, None] == columns[None, :]).astype(jnp.bfloat16)


def standardize_dosage(block_dosage):
    genotype = block_dosage.astype(jnp.float32)
    centred = genotype - jnp.mean(genotype, axis=0, keepdims=True)
    return (centred * lax.rsqrt(jnp.mean(centred * centred, axis=0, keepdims=True) + 1e-06)).astype(
        jnp.bfloat16
    )


def on_device(umi_counts, cell_donors, cell_types, live_cells, dosages):
    total_groups = TYPES * DONORS
    cell_slots = umi_counts.shape[0]
    genes_block = umi_counts.shape[1]
    batch_count = lax.axis_size(BATCH)
    genes_local = genes_block // batch_count
    slot_index = jnp.arange(cell_slots, dtype=jnp.int32)
    alive_mask = slot_index < live_cells[0]
    cell_group = jnp.where(alive_mask, cell_types * DONORS + cell_donors, -1)
    rounded = umi_counts.astype(jnp.bfloat16)
    table = one_hot_rows(cell_group, total_groups)
    pseudo = summed_rows_2(
        lax.dot_general(
            rounded, table, (((0,), (0,)), ((), ())), preferred_element_type=jnp.float32
        ),
        ("batch_0", "batch_1"),
        "batch_2",
        0,
    )
    partial_library = jnp.sum(pseudo, axis=0)
    library = jnp.maximum(one_axis_at_a_time(partial_library, BATCH_GENE), 1.0)
    logged = jnp.log1p(10000.0 * pseudo / library[None, :]).reshape(genes_local, TYPES, DONORS)
    centred = logged - jnp.mean(logged, axis=2, keepdims=True)
    standard = (
        centred * lax.rsqrt(jnp.mean(centred * centred, axis=2, keepdims=True) + 1e-06)
    ).astype(jnp.bfloat16)
    standard_rows = jnp.transpose(standard, (1, 0, 2)).reshape(TYPES * genes_local, DONORS)
    factor = DONORS ** (-0.5)
    geno_local = standardize_dosage(dosages)
    geno_piece = lax.all_gather(geno_local, BATCH, axis=1, tiled=True)
    product = jnp.dot(standard_rows, geno_piece, preferred_element_type=jnp.float32) * factor
    return product.reshape(TYPES, genes_local, geno_piece.shape[1]).astype(jnp.bfloat16)


def solution(mesh):
    torus = Mesh(
        mesh.devices.reshape(4, 4, 2, 4, 2), ("batch_0", "batch_1", "batch_2", "gene_0", "gene_1")
    )
    return jax.shard_map(
        on_device,
        mesh=torus,
        in_specs=(P(BATCH, GENE), P(BATCH), P(BATCH), P(BATCH), P(None, BATCH)),
        out_specs=P(None, GENE_BATCH, None),
        check_vma=False,
    )
```

profile of v0, /device:TPU:32, one launch (start us, length us, event | category | flops | bytes accessed | tf_op | source)
XLA Modules:
  0.0 256.0 jit_solution(15902992954588551847)
XLA Ops:
  8.0 0.7 add_select_fusion
  8.7 12.0 %fusion = f32[3072,1024]{0,1:T(8,128)} fusion(s32[1024]{0:T(1024)S(1)} %add_select_fusion, s32[1024,1024]{1,0:T(8,128)} %param.5), kind=kOutput, calls=%fused_computation.2 | convolution fusion | flops 6446645248 | bytes 16781312 | tf_op jit(solution)/shard_map/dot_general | solution.py:61
  20.7 10.8 %copy.6 = f32[16,2,32,3072]{3,2,0,1:T(8,128)} copy(f32[16,2,32,3072]{3,2,1,0:T(8,128)} %bitcast.21) | data formatting | bytes 25165824 | tf_op jit(solution)/shard_map/reshape;reshape | solution.py:25
  31.5 0.0 reduce-scatter.3.cloned.1.call-update
  31.5 0.0 copy-start
  31.6 0.0 reduce-scatter.5.cloned.1.call-start
  31.6 30.0 %reduce-scatter.3.cloned.1.call-done = f32[16,32,3072]{2,1,0:T(8,128)} async-done(((f32[32,32,3072]{2,1,0:T(8,128)}), f32[16,32,3072]{2,1,0:T(8,128)}) %reduce-scatter.3.cloned.1.call-update) | async-done | bytes 6291472 | tf_op jit(solution)/shard_map/reduce_scatter | solution.py:26
  61.6 0.0 reduce-scatter.5.cloned.1.call-update
  61.6 0.0 all-gather.2.cloned.1.call-start
  61.8 0.6 multiply_convert_fusion.2
  62.4 0.0 all-gather.2.cloned.1.call-update
  62.4 114.4 %reduce-scatter.5.cloned.1.call-done = f32[1,32,3072]{2,1,0:T(8,128)} async-done(((f32[16,32,3072]{2,1,0:T(8,128)}), f32[1,32,3072]{2,1,0:T(8,128)}) %reduce-scatter.5.cloned.1.call-update) | async-done | bytes 393232 | tf_op jit(solution)/shard_map/reduce_scatter | solution.py:27
  176.9 1.0 multiply_bitcast_fusion
  177.9 0.1 copy.8
  178.0 19.5 %psum.35 = f32[3072]{0:T(1024)S(1)} all-reduce(f32[3072]{0:T(1024)S(1)} %get-tuple-element.6), channel_id=1, replica_groups=mesh['batch_0'=4,'batch_1'=4,'batch_2'=2,'gene_0'=4,'gene_1'=2] {'batch_0'}, use_global_device_ids=true, to_apply=%region_3.4 | all-reduce | flops 3072 | bytes 24576 | tf_op jit(solution)/shard_map/psum | solution.py:32
  197.5 15.9 %psum.36 = f32[3072]{0:T(1024)S(1)} all-reduce(f32[3072]{0:T(1024)S(1)} %psum.35), channel_id=1, replica_groups=mesh['batch_0'=4,'batch_1'=4,'batch_2'=2,'gene_0'=4,'gene_1'=2] {'batch_1'}, use_global_device_ids=true, to_apply=%region_4.5 | all-reduce | flops 3072 | bytes 24576 | tf_op jit(solution)/shard_map/psum | solution.py:32
  213.3 3.3 %psum.37 = f32[3072]{0:T(1024)S(1)} all-reduce(f32[3072]{0:T(1024)S(1)} %psum.36), channel_id=1, replica_groups=mesh['batch_0'=4,'batch_1'=4,'batch_2'=2,'gene_0'=4,'gene_1'=2] {'batch_2'}, use_global_device_ids=true, to_apply=%region_5.6 | all-reduce | flops 3072 | bytes 24576 | tf_op jit(solution)/shard_map/psum | solution.py:32
  216.6 16.8 %psum.38 = f32[3072]{0:T(1024)S(1)} all-reduce(f32[3072]{0:T(1024)S(1)} %psum.37), channel_id=1, replica_groups=mesh['batch_0'=4,'batch_1'=4,'batch_2'=2,'gene_0'=4,'gene_1'=2] {'gene_0'}, use_global_device_ids=true, to_apply=%region_6.7 | all-reduce | flops 3072 | bytes 24576 | tf_op jit(solution)/shard_map/psum | solution.py:32
  233.4 8.5 %psum.39 = f32[3072]{0:T(1024)S(1)} all-reduce(f32[3072]{0:T(1024)S(1)} %psum.38), channel_id=1, replica_groups=mesh['batch_0'=4,'batch_1'=4,'batch_2'=2,'gene_0'=4,'gene_1'=2] {'gene_1'}, use_global_device_ids=true, to_apply=%region_7.8 | all-reduce | flops 3072 | bytes 24576 | tf_op jit(solution)/shard_map/psum | solution.py:32
  241.9 0.2 fusion.4
  242.1 0.3 multiply_reduce_fusion
  242.5 0.3 multiply_convert_fusion.1
  242.8 0.0 all-gather.2.cloned.1.call-done
  242.8 5.7 %multiply_convert_fusion = bf16[768,4096]{1,0:T(8,128)(2,1)} fusion(bf16[768,128]{1,0:T(8,128)(2,1)S(1)} %bitcast.25, bf16[128,4096]{1,0:T(8,128)(2,1)} %all-gather.2.cloned.1.call-done), kind=kOutput, calls=%fused_computation | convolution fusion | flops 811597824 | bytes 7536640 | tf_op jit(solution)/shard_map/dot_general | solution.py:79
  (9 shorter events, 0.1 us)
Async XLA Ops:
  7.4 54.2 %reduce-scatter.3.cloned.1.call-start = ((), (), s32[]{:S(2)}) async-start(), calls=%async_computation.2 | async-start | bytes 18874368 | tf_op jit(solution)/shard_map/reduce_scatter | solution.py:26
  31.5 30.1 %copy-start = (s32[128,128]{1,0:T(8,128)S(1)}, s32[128,128]{1,0:T(8,128)}, u32[]{:S(2)}) copy-start(s32[128,128]{1,0:T(8,128)} %param.9) | copy-start | bytes 196612
  31.6 145.3 %reduce-scatter.5.cloned.1.call-start = ((), (), s32[]{:S(2)}) async-start(), calls=%async_computation.3 | async-start | bytes 6684672 | tf_op jit(solution)/shard_map/reduce_scatter | solution.py:27
  61.6 181.2 %all-gather.2.cloned.1.call-start = ((), (), s32[]{:S(2)}) async-start(), calls=%async_computation.4 | async-start | bytes 1081344 | tf_op jit(solution)/shard_map/all_gather | solution.py:78
Sparse Core Ops, SparseCore 0:
  31.7 29.8 reduce-scatter.2
  65.3 111.5 reduce-scatter.4
Sparse Core Ops, SparseCore 1:
  64.6 63.7 all-gather.1
where the time goes:
time: 256 us
  waiting for transfers between devices  145 us (57%)
  blocking collectives  63.9 us (25%)
  matrix products  17.7 us (7%)
  between operations  15.6 us (6%)
  local copies, waits for them, and re-layouts  10.9 us (4%)
  other arithmetic  3.33 us (1%)
    reduce_scatter x1, waiting for transfers between devices, summed_rows_2(): return lax.psum_scatter(tiles, chips, scatter_dimension=0, tiled=True)[0]  114 us
    psum x5, blocking collectives, one_axis_at_a_time(): value = lax.psum(value, axis)  63.9 us
    reduce_scatter x1, waiting for transfers between devices, summed_rows_2(): tiles = lax.psum_scatter(tiles, core, scatter_dimension=0, tiled=True)  30 us
    dot_general x1, matrix products, on_device(): lax.dot_general(rounded, table, (((0,), (0,)), ((), ())), preferred_eleme...  12 us
    another operation x1, local copies, waits for them, and re-layouts, summed_rows_2(): tiles = tiles.reshape(*sizes, *inside).swapaxes(0, 1).reshape(-1, *inside)  10.8 us
    dot_general x1, matrix products, on_device(): jnp.dot(standard_rows, geno_piece, preferred_element_type=jnp.float32)  5.72 us
  transfers between devices with their start and end apart: 3, of which 2 were waited for; matrix products, arithmetic and copies ran while one was open for 1% of the time, Pallas kernels for 0%

commit v1 on v0

--- a/solution.py
+++ b/solution.py
@@ -29,7 +29,7 @@
 
 def one_axis_at_a_time(value, axes):
     for axis in axes:
-        value = lax.psum(value, axis)
+        value = jnp.sum(lax.all_gather(value, axis), axis=0)
     return value
 
 

time: 256 us -> 238 us (0.930)
  blocking collectives: 63.9 us -> 45 us
    psum x5 -> x0, blocking collectives: 63.9 us -> none  [one_axis_at_a_time(): value = lax.psum(value, axis)]
    all_gather x0 -> x5, blocking collectives: none -> 45 us  [one_axis_at_a_time(): value = jnp.sum(lax.all_gather(value, axis), axis=0)]
where the time goes in v1:
time: 238 us; the launch traced here: 237 us
  waiting for transfers between devices  145 us (61%)
  blocking collectives  45 us (19%)
  matrix products  17.7 us (7%)
  between operations  15.6 us (7%)
  local copies, waits for them, and re-layouts  11 us (5%)
  other arithmetic  3.49 us (1%)
    reduce_scatter x1, waiting for transfers between devices, summed_rows_2(): return lax.psum_scatter(tiles, chips, scatter_dimension=0, tiled=True)[0]  114 us
    all_gather x5, blocking collectives, one_axis_at_a_time(): value = jnp.sum(lax.all_gather(value, axis), axis=0)  45 us
    reduce_scatter x1, waiting for transfers between devices, summed_rows_2(): tiles = lax.psum_scatter(tiles, core, scatter_dimension=0, tiled=True)  30 us
    dot_general x1, matrix products, on_device(): lax.dot_general(rounded, table, (((0,), (0,)), ((), ())), preferred_eleme...  12 us
    another operation x1, local copies, waits for them, and re-layouts, summed_rows_2(): tiles = tiles.reshape(*sizes, *inside).swapaxes(0, 1).reshape(-1, *inside)  10.8 us
    dot_general x1, matrix products, on_device(): jnp.dot(standard_rows, geno_piece, preferred_element_type=jnp.float32)  5.72 us
  transfers between devices with their start and end apart: 3, of which 2 were waited for; matrix products, arithmetic and copies ran while one was open for 1% of the time, Pallas kernels for 0%

profile of v1, /device:TPU:32, one launch (start us, length us, event | category | flops | bytes accessed | tf_op | source)
XLA Modules:
  0.0 237.4 jit_solution(6640719165067442575)
XLA Ops:
  8.0 0.7 add_select_fusion
  8.7 12.0 %fusion = f32[3072,1024]{0,1:T(8,128)} fusion(s32[1024]{0:T(1024)S(1)} %add_select_fusion, s32[1024,1024]{1,0:T(8,128)} %param.5), kind=kOutput, calls=%fused_computation.2 | convolution fusion | flops 6446645248 | bytes 16781312 | tf_op jit(solution)/shard_map/dot_general | solution.py:61
  20.7 10.8 %copy.10 = f32[16,2,32,3072]{3,2,0,1:T(8,128)} copy(f32[16,2,32,3072]{3,2,1,0:T(8,128)} %bitcast.21) | data formatting | bytes 25165824 | tf_op jit(solution)/shard_map/reshape;reshape | solution.py:25
  31.5 0.0 reduce-scatter.3.cloned.1.call-update
  31.5 0.0 copy-start
  31.6 0.0 reduce-scatter.5.cloned.1.call-start
  31.6 30.0 %reduce-scatter.3.cloned.1.call-done = f32[16,32,3072]{2,1,0:T(8,128)} async-done(((f32[32,32,3072]{2,1,0:T(8,128)}), f32[16,32,3072]{2,1,0:T(8,128)}) %reduce-scatter.3.cloned.1.call-update) | async-done | bytes 6291472 | tf_op jit(solution)/shard_map/reduce_scatter | solution.py:26
  61.6 0.0 reduce-scatter.5.cloned.1.call-update
  61.6 0.0 all-gather.7.cloned.1.call-start
  61.8 0.6 multiply_convert_fusion.2
  62.4 0.0 all-gather.7.cloned.1.call-update
  62.4 114.4 %reduce-scatter.5.cloned.1.call-done = f32[1,32,3072]{2,1,0:T(8,128)} async-done(((f32[16,32,3072]{2,1,0:T(8,128)}), f32[1,32,3072]{2,1,0:T(8,128)}) %reduce-scatter.5.cloned.1.call-update) | async-done | bytes 393232 | tf_op jit(solution)/shard_map/reduce_scatter | solution.py:27
  176.9 1.0 multiply_bitcast_fusion
  177.9 13.7 %all-gather = f32[12288]{0:T(1024)S(1)} all-gather(f32[3072]{0:T(1024)S(1)} %get-tuple-element.6), channel_id=2, replica_groups=mesh['batch_0'=4,'batch_1'=4,'batch_2'=2,'gene_0'=4,'gene_1'=2] {'batch_0'}, dimensions={0}, use_global_device_ids=true | all-gather | bytes 61440 | tf_op jit(solution)/shard_map/all_gather | solution.py:32
  191.7 13.1 %all-gather.1 = f32[12288]{0:T(1024)S(1)} all-gather(f32[3072]{0:T(1024)S(1)} %reduce_sum.91), channel_id=3, replica_groups=mesh['batch_0'=4,'batch_1'=4,'batch_2'=2,'gene_0'=4,'gene_1'=2] {'batch_1'}, dimensions={0}, use_global_device_ids=true | all-gather | bytes 61440 | tf_op jit(solution)/shard_map/all_gather | solution.py:32
  204.8 1.8 all-gather.2
  206.7 12.0 %all-gather.3 = f32[12288]{0:T(1024)S(1)} all-gather(f32[3072]{0:T(1024)S(1)} %reduce_sum.93), channel_id=5, replica_groups=mesh['batch_0'=4,'batch_1'=4,'batch_2'=2,'gene_0'=4,'gene_1'=2] {'gene_0'}, dimensions={0}, use_global_device_ids=true | all-gather | bytes 61440 | tf_op jit(solution)/shard_map/all_gather | solution.py:32
  218.7 4.4 %all-gather.4 = f32[6144]{0:T(1024)S(1)} all-gather(f32[3072]{0:T(1024)S(1)} %reduce_sum.94), channel_id=6, replica_groups=mesh['batch_0'=4,'batch_1'=4,'batch_2'=2,'gene_0'=4,'gene_1'=2] {'gene_1'}, dimensions={0}, use_global_device_ids=true | all-gather | bytes 36864 | tf_op jit(solution)/shard_map/all_gather | solution.py:32
  223.2 0.1 copy.12
  223.3 0.2 fusion.4
  223.5 0.3 multiply_reduce_fusion
  223.9 0.3 multiply_convert_fusion.1
  224.2 0.0 all-gather.7.cloned.1.call-done
  224.2 5.7 %multiply_convert_fusion = bf16[768,4096]{1,0:T(8,128)(2,1)} fusion(bf16[768,128]{1,0:T(8,128)(2,1)S(1)} %bitcast.25, bf16[128,4096]{1,0:T(8,128)(2,1)} %all-gather.7.cloned.1.call-done), kind=kOutput, calls=%fused_computation | convolution fusion | flops 811597824 | bytes 7536640 | tf_op jit(solution)/shard_map/dot_general | solution.py:79
  (19 shorter events, 0.4 us)
Async XLA Ops:
  7.4 54.2 %reduce-scatter.3.cloned.1.call-start = ((), (), s32[]{:S(2)}) async-start(), calls=%async_computation.2 | async-start | bytes 18874368 | tf_op jit(solution)/shard_map/reduce_scatter | solution.py:26
  31.5 30.1 %copy-start = (s32[128,128]{1,0:T(8,128)S(1)}, s32[128,128]{1,0:T(8,128)}, u32[]{:S(2)}) copy-start(s32[128,128]{1,0:T(8,128)} %param.9) | copy-start | bytes 196612
  31.6 145.3 %reduce-scatter.5.cloned.1.call-start = ((), (), s32[]{:S(2)}) async-start(), calls=%async_computation.3 | async-start | bytes 6684672 | tf_op jit(solution)/shard_map/reduce_scatter | solution.py:27
  61.6 162.6 %all-gather.7.cloned.1.call-start = ((), (), s32[]{:S(2)}) async-start(), calls=%async_computation.4 | async-start | bytes 1081344 | tf_op jit(solution)/shard_map/all_gather | solution.py:78
Sparse Core Ops, SparseCore 0:
  31.7 29.8 reduce-scatter.2
  65.3 111.5 reduce-scatter.4
Sparse Core Ops, SparseCore 1:
  64.6 63.7 all-gather.6
